TPU v7x, 32 devices: a whole 2x2x4 slice. The times are simulated.
32 devices in a mesh: blk: 16 (over z, y, core), head: 2 (over x).
Axes of the slice: x: 2, y: 2, z: 4, core: 2. Of those that a mesh axis runs over, the one named last changes fastest.
Arguments:
- queries: bfloat16 [8192, 16, 128], P('blk', 'head'), may hold values from -6 to 6
- out_grad: bfloat16 [8192, 16, 128], P('blk', 'head'), may hold values from -6 to 6
- outputs: bfloat16 [8192, 16, 128], P('blk', 'head'), may hold values from -6 to 6
- key_vectors: bfloat16 [8192, 128], P('blk'), may hold values from -6 to 6
- value_vectors: bfloat16 [8192, 128], P('blk'), may hold values from -6 to 6
- logsumexp: float32 [8192, 16], P('blk', 'head'), may hold values from 4 to 7
- positions: int32 [8192], P('blk'), may hold values from 0 to 8191, as said below
- doc_start: int32 [8192], P('blk'), may hold values from 0 to 8191, as said below
Outputs:
- query_grad: bfloat16 [8192, 16, 128], P('blk', 'head')
- key_grad: bfloat16 [8192, 128], P('blk')
- value_grad: bfloat16 [8192, 128], P('blk')
Inputs may be any that keep to these rules, and one draw needn't show every extreme that they name: positions is a permutation of 0 to 8191; row r holds position (r mod 512) * 16 + sigma(r div 512), sigma a permutation of the blocks of 512 rows. doc_start of a row is the first position of the document that holds the row's position; documents are runs of consecutive positions, the first starting at 0, and the last position starts a document of its own.
All inputs are finite; a program needn't handle non-finite values.
Results may differ from a plain program's by a relative error of at most 0.0063.
Values may be sent and summed in bfloat16 or wider, within the bound.
A program may use at most 64 MiB of HBM per device.

v0:
```python
import functools
import math

import jax
import jax.numpy as jnp
from jax import lax
from jax.experimental import pallas as pl
from jax.experimental.pallas import tpu as pltpu
from jax.sharding import PartitionSpec as P

STEPS = 4
TILE = 64
CHUNKS = 4
LOG2E = math.log2(math.e)
MESH = pl.DeviceIdType.MESH
VMEM_SPEC = pl.BlockSpec(memory_space=pltpu.VMEM)


def places(n):
    b = lax.axis_index("blk")
    h = lax.axis_index("head")
    even = lax.rem(b, 2) == 0
    partner = jnp.where(even, b + 1, b - 1)

    def at(d):
        return lax.rem(b + d + n, n)

    return b, h, even, partner, at


def greet(n):
    b, h, even, partner, at = places(n)
    barrier = pltpu.get_barrier_semaphore()
    for d in (-3, -2, -1, 1, 2, 3):
        pl.semaphore_signal(barrier, inc=1, device_id=(at(d), h), device_id_type=MESH)
    pl.semaphore_signal(barrier, inc=1, device_id=(b, 1 - h), device_id_type=MESH)
    pl.semaphore_wait(barrier, 7)


def gather_kernel(
    n, first_ref, k_ref, v_ref, lse_ref, start_ref, last_ref, g_hbm, o_hbm,
    kall, vall, pos_all, table, g_ref, o_ref, pos_ref, send, recv, local, wide,
):
    b, h, even, partner, at = places(n)
    rows = k_ref.shape[0]
    half = rows // 2
    mine = pl.ds(pl.multiple_of(h * half, half), half)
    other = pl.ds(pl.multiple_of((1 - h) * half, half), half)
    pairs = ((k_ref, kall), (v_ref, vall))

    def copy(src, dst, kind, j, who):
        return pltpu.make_async_remote_copy(
            src_ref=src,
            dst_ref=dst,
            send_sem=send.at[kind, j],
            recv_sem=recv.at[kind, j],
            device_id=who,
            device_id_type=MESH,
        )

    own = [
        pltpu.make_async_copy(src, dst.at[0], local.at[j])
        for j, (src, dst) in enumerate(pairs)
    ]
    wides = [
        pltpu.make_async_copy(src, dst, wide.at[j])
        for j, (src, dst) in enumerate(((g_hbm, g_ref), (o_hbm, o_ref)))
    ]
    pos_ref[...] = jnp.full(pos_ref.shape, first_ref[0], pos_ref.dtype)
    pos_all[0] = jnp.full(pos_ref.shape, first_ref[0], pos_ref.dtype)
    for c in own + wides:
        c.start()
    greet(n)
    pslot = jnp.where(even, 1, 3)
    qslot = jnp.where(even, 3, 1)
    first, third, near = [], [], []
    for j, (src, dst) in enumerate(pairs):
        first.append(copy(src.at[mine], dst.at[2, mine], 0, j, (at(-2), h)))
        third.append(copy(src.at[mine], dst.at[3, mine], 1, j, (at(-3), h)))
        near.append(copy(src, dst.at[1], 2, j, (partner, h)))
    for j in range(2):
        first[j].start()

        @pl.when(even)
        def _():
            third[j].start()

        @pl.when(jnp.logical_not(even))
        def _():
            near[j].start()

    marks = [
        copy(pos_ref, pos_all.at[d], 7 + d // 3, d % 3, (at(-d), h)) for d in range(1, STEPS)
    ]
    for c in marks:
        c.start()

    for c in wides:
        c.wait()
    heads, tokens = lse_ref.shape
    block = TILE * heads
    spread = (
        lax.broadcasted_iota(jnp.int32, (TILE, block), 1) // heads
        == lax.broadcasted_iota(jnp.int32, (TILE, block), 0)
    ).astype(jnp.bfloat16)
    choose = (
        lax.broadcasted_iota(jnp.int32, (heads, block), 1) % heads
        == lax.broadcasted_iota(jnp.int32, (heads, block), 0)
    )

    def spread_whole(values):
        upper = values // 256
        lower = values - upper * 256
        up, low = (
            jnp.dot(
                jnp.broadcast_to(part.astype(jnp.float32), (8, TILE)).astype(jnp.bfloat16),
                spread,
                preferred_element_type=jnp.float32,
            )
            for part in (upper, lower)
        )
        return (up * 256.0 + low)[0:1]

    ones = jnp.ones((8, g_ref.shape[1]), jnp.bfloat16)
    contract = (((1,), (1,)), ((), ()))
    for c in range(g_ref.shape[0] // block):
        r = pl.ds(c * block, block)
        product = g_ref[r].astype(jnp.float32) * o_ref[r].astype(jnp.float32)
        upper = product.astype(jnp.bfloat16)
        lower = (product - upper.astype(jnp.float32)).astype(jnp.bfloat16)
        delta = lax.dot_general(
            ones, upper, contract, preferred_element_type=jnp.float32
        ) + lax.dot_general(ones, lower, contract, preferred_element_type=jnp.float32)
        table[0:1, r] = delta[0:1]
        rest = lse_ref[:, c * TILE : (c + 1) * TILE] * LOG2E
        lse = jnp.zeros((heads, block), jnp.float32)
        for _ in range(3):
            part = rest.astype(jnp.bfloat16)
            rest = rest - part.astype(jnp.float32)
            lse += jnp.dot(part, spread, preferred_element_type=jnp.float32)
        table[1:2, r] = jnp.sum(jnp.where(choose, lse, 0.0), axis=0, keepdims=True)
        at = slice(c * TILE, (c + 1) * TILE)
        table[2:3, r] = spread_whole(start_ref[:, at])
        table[3:4, r] = spread_whole(last_ref[:, at])

    side, side3, fwd, fwd2 = [], [], [], []
    for j, (src, dst) in enumerate(pairs):
        side.append(copy(dst.at[2, mine], dst.at[2, mine], 3, j, (b, 1 - h)))
        side3.append(copy(dst.at[3, mine], dst.at[3, mine], 4, j, (b, 1 - h)))
        fwd.append(copy(dst.at[2, mine], dst.at[pslot, mine], 5, j, (partner, h)))
        fwd2.append(copy(dst.at[2, other], dst.at[pslot, other], 6, j, (partner, h)))
    for j in range(2):
        first[j].wait_recv()
        side[j].start()
        fwd[j].start()
    for j in range(2):

        @pl.when(jnp.logical_not(even))
        def _():
            third[j].wait_recv()
            side3[j].start()

    for j in range(2):
        side[j].wait_recv()
        fwd2[j].start()
    for j in range(2):
        fwd[j].wait_recv()
        fwd2[j].wait_recv()

        @pl.when(even)
        def _():
            near[j].wait_recv()
            third[j].wait_send()

        @pl.when(jnp.logical_not(even))
        def _():
            side3[j].wait_recv()
            near[j].wait_send()
            side3[j].wait_send()

        first[j].wait_send()
        side[j].wait_send()
        fwd[j].wait_send()
        fwd2[j].wait_send()
    for c in own + marks:
        c.wait()


def gather(n, keys, values, logsumexp, positions, doc_start, g, o):
    rows, width = keys.shape
    shape = jax.ShapeDtypeStruct((STEPS, rows, width), keys.dtype)
    mark = (8, width)
    return pl.pallas_call(
        functools.partial(gather_kernel, n),
        out_shape=(
            shape,
            shape,
            jax.ShapeDtypeStruct((STEPS,) + mark, positions.dtype),
            jax.ShapeDtypeStruct((4, g.shape[0]), jnp.float32),
        ),
        in_specs=[pl.BlockSpec(memory_space=pltpu.SMEM)]
        + [VMEM_SPEC] * 5
        + [pl.BlockSpec(memory_space=pltpu.HBM)] * 2,
        out_specs=(VMEM_SPEC,) * 4,
        scratch_shapes=[
            pltpu.VMEM(g.shape, g.dtype),
            pltpu.VMEM(g.shape, g.dtype),
            pltpu.VMEM(mark, positions.dtype),
            pltpu.SemaphoreType.DMA((9, 3)),
            pltpu.SemaphoreType.DMA((9, 3)),
            pltpu.SemaphoreType.DMA((2,)),
            pltpu.SemaphoreType.DMA((2,)),
        ],
        compiler_params=pltpu.CompilerParams(
            collective_id=0, has_side_effects=True, vmem_limit_bytes=16 << 20
        ),
        cost_estimate=pl.CostEstimate(
            flops=32 * g.size, bytes_accessed=16 * g.size, transcendentals=0
        ),
        name="gather_kv",
    )(
        positions,
        keys,
        values,
        logsumexp.T,
        doc_start.reshape(1, -1),
        positions.reshape(1, -1),
        g,
        o,
    )


def compute_kernel(
    n, tile, start_ref, q_ref, g_ref, table, k_ref, v_ref, marks_ref,
    dq_ref, dk_ref, dv_ref, dk_acc, dv_acc, dq_acc, p_buf, ds_buf, kp_buf,
):
    steps, tokens, width = k_ref.shape
    count = tokens // tile
    block = q_ref.shape[0] // count
    keys = steps * tile
    scaling = width ** (-0.5)
    contract = (((1,), (1,)), ((), ()))

    dk_acc[...] = jnp.zeros_like(dk_acc)
    dv_acc[...] = jnp.zeros_like(dv_acc)
    dq_acc[...] = jnp.zeros_like(dq_acc)
    ramp = lax.broadcasted_iota(jnp.int32, (tile, width), 0) * n
    for s in range(steps):
        kp_buf[s * tile : (s + 1) * tile, :] = (
            ramp + marks_ref[s, 0:1, :]
        ).astype(jnp.float32)

    def lowest(i):
        return start_ref[i * tile] // (n * tile)

    def probs(i, t):
        at = pl.ds(pl.multiple_of(t * tile, tile), tile)
        r = pl.ds(pl.multiple_of(i * block, block), block)
        k = k_ref[:, at, :].reshape(keys, width)
        v = v_ref[:, at, :].reshape(keys, width)
        moved = (t * (tile * n)).astype(jnp.float32)
        start = table[2:3, r] - moved
        last = table[3:4, r] - moved
        kp = jnp.concatenate([kp_buf[...]] * (block // width), axis=1)
        s = lax.dot_general(k, q_ref[r, :], contract, preferred_element_type=jnp.float32)
        dp = lax.dot_general(v, g_ref[r, :], contract, preferred_element_type=jnp.float32)
        ok = (kp <= last) & (kp >= start)
        p = jnp.where(ok, jnp.exp2(s * (scaling * LOG2E) - table[1:2, r]), 0.0)
        return p.astype(jnp.bfloat16), (p * (dp - table[0:1, r])).astype(jnp.bfloat16)

    def add_grads(i, t):
        at = pl.ds(pl.multiple_of(t * tile, tile), tile)
        r = pl.ds(pl.multiple_of(i * block, block), block)
        k = k_ref[:, at, :].reshape(keys, width)
        ds = ds_buf[...]
        dv = jnp.dot(p_buf[...], g_ref[r, :], preferred_element_type=jnp.float32)
        dk = jnp.dot(ds, q_ref[r, :], preferred_element_type=jnp.float32)
        dv_acc[:, at, :] += dv.reshape(steps, tile, width)
        dk_acc[:, at, :] += dk.reshape(steps, tile, width)
        dq_acc[r, :] += lax.dot_general(
            ds, k, (((0,), (0,)), ((), ())), preferred_element_type=jnp.float32
        )

    def put(pair):
        p_buf[...], ds_buf[...] = pair

    total = lax.fori_loop(0, count, lambda i, c: c + i - lowest(i) + 1, 0)
    put(probs(0, lowest(0)))

    def body(_, spot):
        i, t = spot
        done = t >= i
        new_i = jnp.where(done, i + 1, i)
        new_t = jnp.where(done, lowest(new_i), t + 1)
        pair = probs(new_i, new_t)
        add_grads(i, t)
        put(pair)
        return new_i, new_t

    i, t = lax.fori_loop(1, total, body, (jnp.int32(0), lowest(0)))
    add_grads(i, t)
    dq_ref[...] = (dq_acc[...] * scaling).astype(dq_ref.dtype)
    dk_ref[...] = (dk_acc[...] * scaling).astype(dk_ref.dtype)
    dv_ref[...] = dv_acc[...].astype(dv_ref.dtype)


def compute(n, tile, starts, q, g, table, kall, vall, marks):
    steps, tokens, width = kall.shape
    block = q.shape[0] // (tokens // tile)
    part = jax.ShapeDtypeStruct(kall.shape, jnp.bfloat16)
    return pl.pallas_call(
        functools.partial(compute_kernel, n, tile),
        out_shape=(jax.ShapeDtypeStruct(q.shape, q.dtype), part, part),
        in_specs=[pl.BlockSpec(memory_space=pltpu.SMEM)] + [VMEM_SPEC] * 6,
        out_specs=(VMEM_SPEC,) * 3,
        scratch_shapes=[
            pltpu.VMEM(kall.shape, jnp.float32),
            pltpu.VMEM(kall.shape, jnp.float32),
            pltpu.VMEM(q.shape, jnp.float32),
            pltpu.VMEM((steps * tile, block), jnp.bfloat16),
            pltpu.VMEM((steps * tile, block), jnp.bfloat16),
            pltpu.VMEM((steps * tile, width), jnp.float32),
        ],
        compiler_params=pltpu.CompilerParams(vmem_limit_bytes=28 << 20),
        cost_estimate=pl.CostEstimate(
            flops=10 * q.shape[0] * steps * tokens * width // 2,
            bytes_accessed=6 * q.size,
            transcendentals=q.shape[0] * steps * tokens // 2,
        ),
        name="block_grads",
    )(starts, q, g, table, kall, vall, marks)


def reduce_kernel(
    n, pk, pv, total_k, total_v, last_k, last_v, near, both, far, mid, guest, send, recv
):
    b, h, even, partner, at = places(n)
    rows = pk.shape[1]
    size = rows // CHUNKS
    parts = (pk, pv)
    total = (total_k, total_v)
    last = (last_k, last_v)
    odd = jnp.logical_not(even)

    def copy(src, dst, kind, j, c, who):
        return pltpu.make_async_remote_copy(
            src_ref=src,
            dst_ref=dst,
            send_sem=send.at[kind, j, c],
            recv_sem=recv.at[kind, j, c],
            device_id=who,
            device_id_type=MESH,
        )

    greet(n)
    work = [(j, c, pl.ds(c * size, size)) for c in range(CHUNKS) for j in range(2)]
    give, own, skip, hop, side = {}, {}, {}, {}, {}
    gslot = jnp.where(even, 3, 1)
    for j, c, r in work:
        give[j, c] = copy(parts[j].at[gslot, r], near.at[j, r], 0, j, c, (partner, h))
        own[j, c] = copy(parts[j].at[1, r], both.at[j, r], 1, j, c, (partner, h))
        skip[j, c] = copy(parts[j].at[3, r], far.at[j, r], 2, j, c, (at(3), h))
        hop[j, c] = copy(mid.at[j, r], guest.at[j, r], 3, j, c, (at(2), h))
        side[j, c] = copy(total[j].at[r], last[j].at[r], 4, j, c, (b, 1 - h))
        give[j, c].start()
    for j, c, r in work:
        give[j, c].wait_recv()
        mid[j, r] = (parts[j][2, r].astype(jnp.float32) + near[j, r].astype(jnp.float32)).astype(mid.dtype)
        hop[j, c].start()

        @pl.when(odd)
        def _():
            skip[j, c].start()

        @pl.when(even)
        def _():
            own[j, c].start()

    for j, c, r in work:
        hop[j, c].wait_recv()
        acc = parts[j][0, r].astype(jnp.float32) + guest[j, r].astype(jnp.float32)

        @pl.when(even)
        def _():
            skip[j, c].wait_recv()
            total[j][r] = (acc + far[j, r].astype(jnp.float32)).astype(mid.dtype)

        @pl.when(odd)
        def _():
            own[j, c].wait_recv()
            total[j][r] = (acc + both[j, r].astype(jnp.float32)).astype(mid.dtype)

        side[j, c].start()
    for j, c, r in work:
        side[j, c].wait_recv()
    for j, c, r in work:
        give[j, c].wait_send()
        hop[j, c].wait_send()
        side[j, c].wait_send()

        @pl.when(odd)
        def _():
            skip[j, c].wait_send()

        @pl.when(even)
        def _():
            own[j, c].wait_send()


def reduce_parts(n, pk, pv):
    steps, rows, width = pk.shape
    out = jax.ShapeDtypeStruct((rows, width), jnp.bfloat16)
    buf = pltpu.VMEM((2, rows, width), jnp.bfloat16)
    return pl.pallas_call(
        functools.partial(reduce_kernel, n),
        out_shape=(out,) * 4,
        in_specs=[VMEM_SPEC] * 2,
        out_specs=(VMEM_SPEC,) * 4,
        scratch_shapes=[
            buf,
            buf,
            buf,
            buf,
            buf,
            pltpu.SemaphoreType.DMA((5, 2, CHUNKS)),
            pltpu.SemaphoreType.DMA((5, 2, CHUNKS)),
        ],
        compiler_params=pltpu.CompilerParams(
            collective_id=1, has_side_effects=True, vmem_limit_bytes=12 << 20
        ),
        name="reduce_parts",
    )(pk, pv)


def on_device(
    n, queries, out_grad, outputs, key_vectors, value_vectors, logsumexp, positions, doc_start
):
    tokens, heads, width = queries.shape
    q = queries.reshape(-1, width)
    g = out_grad.reshape(-1, width)
    kall, vall, marks, table = gather(
        n, key_vectors, value_vectors, logsumexp, positions, doc_start, g, outputs.reshape(-1, width)
    )
    dq, pk, pv = compute(n, TILE, doc_start, q, g, table, kall, vall, marks)
    total_k, total_v, last_k, last_v = reduce_parts(n, pk, pv)
    dk = (total_k.astype(jnp.float32) + last_k.astype(jnp.float32)).astype(jnp.bfloat16)
    dv = (total_v.astype(jnp.float32) + last_v.astype(jnp.float32)).astype(jnp.bfloat16)
    return dq.reshape(queries.shape), dk, dv


def solution(mesh):
    n = mesh.shape["blk"]
    in_specs = (
        P("blk", "head", None),
        P("blk", "head", None),
        P("blk", "head", None),
        P("blk", None),
        P("blk", None),
        P("blk", "head"),
        P("blk"),
        P("blk"),
    )
    out_specs = (P("blk", "head", None), P("blk", None), P("blk", None))
    return jax.shard_map(
        functools.partial(on_device, n),
        mesh=mesh,
        in_specs=in_specs,
        out_specs=out_specs,
        check_vma=False,
    )
```

profile of v0, /device:TPU:0, one launch (start us, length us, event | category | flops | bytes accessed | tf_op | source)
XLA Modules:
  0.0 55.2 jit_solution(7059831179895161704)
XLA Ops:
  0.6 0.0 copy-start.7
  0.6 0.0 copy-start.6
  0.7 0.7 %copy-done.7 = s32[512]{0:T(512)S(1)} copy-done((s32[512]{0:T(512)S(1)}, s32[512]{0:T(512)}, u32[]{:S(2)}) %copy-start.7) | copy-done | bytes 2072
  1.3 0.0 copy-done.6
  1.3 0.0 copy-start
  1.3 1.2 %copy-done = bf16[512,8,128]{2,1,0:T(8,128)(2,1)S(1)} copy-done((bf16[512,8,128]{2,1,0:T(8,128)(2,1)S(1)}, bf16[512,8,128]{2,1,0:T(8,128)(2,1)}, u32[]{:S(2)}) %copy-start) | copy-done | bytes 1048600
  2.6 0.0 copy-start.1
  2.6 1.2 %copy-done.1 = bf16[512,8,128]{2,1,0:T(8,128)(2,1)S(1)} copy-done((bf16[512,8,128]{2,1,0:T(8,128)(2,1)S(1)}, bf16[512,8,128]{2,1,0:T(8,128)(2,1)}, u32[]{:S(2)}) %copy-start.1) | copy-done | bytes 1048600
  3.8 0.0 copy-start.3
  3.8 0.9 %copy-done.3 = bf16[512,128]{1,0:T(8,128)(2,1)S(1)} copy-done((bf16[512,128]{1,0:T(8,128)(2,1)S(1)}, bf16[512,128]{1,0:T(8,128)(2,1)}, u32[]{:S(2)}) %copy-start.3) | copy-done | bytes 131096
  4.7 0.0 copy-start.4
  4.7 0.9 %copy-done.4 = bf16[512,128]{1,0:T(8,128)(2,1)S(1)} copy-done((bf16[512,128]{1,0:T(8,128)(2,1)S(1)}, bf16[512,128]{1,0:T(8,128)(2,1)}, u32[]{:S(2)}) %copy-start.4) | copy-done | bytes 131096
  5.6 0.0 copy-start.5
  5.6 0.7 %copy-done.5 = f32[512,8]{0,1:T(8,128)S(1)} copy-done((f32[512,8]{0,1:T(8,128)S(1)}, f32[512,8]{0,1:T(8,128)}, u32[]{:S(2)}) %copy-start.5) | copy-done | bytes 16408
  6.3 0.0 copy-start.2
  6.3 0.0 copy-start.8
  6.3 16.5 %gather_kv.1 = (bf16[4,512,128]{2,1,0:T(8,128)(2,1)S(1)}, bf16[4,512,128]{2,1,0:T(8,128)(2,1)S(1)}, s32[4,8,128]{2,1,0:T(8,128)S(1)}, f32[4,4096]{1,0:T(4,128)S(1)}) custom-call(s32[512]{0:T(512)S(1)} %copy-done.6, bf16[512,128]{1,0:T(8,128)(2,1)S(1)} %copy-done.3, bf16[512,128]{1,0:T(8,128)(2,1)S(1)} %copy-done.4, f32[8,512]{1,0:T(8,128)S(1)} %bitcast.10, ...), custom_call_target="tpu_custom_call" | custom-call | flops 16777216 | bytes 8388608 | tf_op jit(solution)/shard_map/gather_kv/pallas_call | solution.py:193
  22.8 0.0 copy-done.2
  22.8 0.0 copy-done.8
  22.8 12.9 %block_grads.1 = (bf16[4096,128]{1,0:T(8,128)(2,1)}, bf16[4,512,128]{2,1,0:T(8,128)(2,1)S(1)}, bf16[4,512,128]{2,1,0:T(8,128)(2,1)S(1)}) custom-call(s32[512]{0:T(512)S(1)} %copy-done.7, bf16[4096,128]{1,0:T(8,128)(2,1)S(1)} %bitcast.13, bf16[4096,128]{1,0:T(8,128)(2,1)S(1)} %bitcast.9, f32[4,4096]{1,0:T(4,128)S(1)} %get-tuple-element.14.table, ...), custom_call_target="tpu_custom_call" | custom-call | flops 5368709120 | bytes 3145728 | tf_op jit(solution)/shard_map/block_grads/pallas_call | solution.py:311
  35.7 18.7 %reduce_parts.1 = (bf16[512,128]{1,0:T(8,128)(2,1)S(1)}, bf16[512,128]{1,0:T(8,128)(2,1)S(1)}, bf16[512,128]{1,0:T(8,128)(2,1)S(1)}, bf16[512,128]{1,0:T(8,128)(2,1)S(1)}) custom-call(bf16[4,512,128]{2,1,0:T(8,128)(2,1)S(1)} %get-tuple-element.19.pk, bf16[4,512,128]{2,1,0:T(8,128)(2,1)S(1)} %get-tuple-element.20.pv), custom_call_target="tpu_custom_call" | custom-call | tf_op jit(solution)/shard_map/reduce_parts/pallas_call | solution.py:414
  54.5 0.8 %add_convert_fusion = (bf16[512,128]{1,0:T(8,128)(2,1)}, bf16[512,128]{1,0:T(8,128)(2,1)}) fusion(bf16[512,128]{1,0:T(8,128)(2,1)S(1)} %get-tuple-element.24, bf16[512,128]{1,0:T(8,128)(2,1)S(1)} %get-tuple-element.23, bf16[512,128]{1,0:T(8,128)(2,1)S(1)} %get-tuple-element.22, bf16[512,128]{1,0:T(8,128)(2,1)S(1)} %get-tuple-element.21), kind=kLoop, calls=%fused_computation | loop fusion | flops 524288 | bytes 786432 | tf_op jit(solution)/shard_map/convert_element_type | solution.py:447
Async XLA Ops:
  0.6 0.7 %copy-start.7 = (s32[512]{0:T(512)S(1)}, s32[512]{0:T(512)}, u32[]{:S(2)}) copy-start(s32[512]{0:T(512)} %start_ref.1) | copy-start | bytes 6148
  0.6 0.7 %copy-start.6 = (s32[512]{0:T(512)S(1)}, s32[512]{0:T(512)}, u32[]{:S(2)}) copy-start(s32[512]{0:T(512)} %first_ref.1) | copy-start | bytes 6148
  1.3 1.2 %copy-start = (bf16[512,8,128]{2,1,0:T(8,128)(2,1)S(1)}, bf16[512,8,128]{2,1,0:T(8,128)(2,1)}, u32[]{:S(2)}) copy-start(bf16[512,8,128]{2,1,0:T(8,128)(2,1)} %param.10) | copy-start | bytes 3145732
  2.6 1.2 %copy-start.1 = (bf16[512,8,128]{2,1,0:T(8,128)(2,1)S(1)}, bf16[512,8,128]{2,1,0:T(8,128)(2,1)}, u32[]{:S(2)}) copy-start(bf16[512,8,128]{2,1,0:T(8,128)(2,1)} %param.9) | copy-start | bytes 3145732
  3.8 0.9 %copy-start.3 = (bf16[512,128]{1,0:T(8,128)(2,1)S(1)}, bf16[512,128]{1,0:T(8,128)(2,1)}, u32[]{:S(2)}) copy-start(bf16[512,128]{1,0:T(8,128)(2,1)} %k_ref.1) | copy-start | bytes 393220
  4.7 0.9 %copy-start.4 = (bf16[512,128]{1,0:T(8,128)(2,1)S(1)}, bf16[512,128]{1,0:T(8,128)(2,1)}, u32[]{:S(2)}) copy-start(bf16[512,128]{1,0:T(8,128)(2,1)} %v_ref.1) | copy-start | bytes 393220
  5.6 0.7 %copy-start.5 = (f32[512,8]{0,1:T(8,128)S(1)}, f32[512,8]{0,1:T(8,128)}, u32[]{:S(2)}) copy-start(f32[512,8]{0,1:T(8,128)} %param.13) | copy-start | bytes 49156
  6.3 16.5 %copy-start.2 = (bf16[512,8,128]{2,1,0:T(8,128)(2,1)S(1)}, bf16[512,8,128]{2,1,0:T(8,128)(2,1)}, u32[]{:S(2)}) copy-start(bf16[512,8,128]{2,1,0:T(8,128)(2,1)} %param.9) | copy-start | bytes 3145732
  6.3 16.5 %copy-start.8 = (bf16[512,8,128]{2,1,0:T(8,128)(2,1)S(1)}, bf16[512,8,128]{2,1,0:T(8,128)(2,1)}, u32[]{:S(2)}) copy-start(bf16[512,8,128]{2,1,0:T(8,128)(2,1)} %param.8) | copy-start | bytes 3145732
where the time goes:
time: 55.6 us; the launch traced here: 55.2 us
  Pallas kernels  48.1 us (87%)
  local copies, waits for them, and re-layouts  5.66 us (10%)
  other arithmetic  0.77 us (1%)
  between operations  0.69 us (1%)
    pallas_call x1, Pallas kernels, reduce_parts(): pl.pallas_call(functools.partial(reduce_kernel, n), out_shape=(out,) * 4,...  18.7 us
    pallas_call x1, Pallas kernels, gather(): pl.pallas_call(functools.partial(gather_kernel, n), out_shape=(shape, sha...  16.5 us
    pallas_call x1, Pallas kernels, compute(): pl.pallas_call(functools.partial(compute_kernel, n, tile), out_shape=(jax...  12.9 us
    unnamed x18, local copies, waits for them, and re-layouts  5.66 us

commit v1 on v0

v1 whole, which is shorter than its diff:
```python
import functools
import math

import jax
import jax.numpy as jnp
from jax import lax
from jax.experimental import pallas as pl
from jax.experimental.pallas import tpu as pltpu
from jax.sharding import PartitionSpec as P

STEPS = 4
TILE = 64
CHUNK = 128
LOG2E = math.log2(math.e)
MESH = pl.DeviceIdType.MESH
VMEM_SPEC = pl.BlockSpec(memory_space=pltpu.VMEM)
ANY_SPEC = pl.BlockSpec(memory_space=pl.ANY)
ROWS = (((1,), (1,)), ((), ()))
COLS = (((0,), (0,)), ((), ()))


def places(n):
    b = lax.axis_index("blk")
    h = lax.axis_index("head")
    even = lax.rem(b, 2) == 0
    partner = jnp.where(even, b + 1, b - 1)

    def at(d):
        return lax.rem(b + d + n, n)

    return b, h, even, partner, at


def greet(n):
    b, h, even, partner, at = places(n)
    barrier = pltpu.get_barrier_semaphore()
    for d in (-3, -2, -1, 1, 2, 3):
        pl.semaphore_signal(barrier, inc=1, device_id=(at(d), h), device_id_type=MESH)
    pl.semaphore_signal(barrier, inc=1, device_id=(b, 1 - h), device_id_type=MESH)
    pl.semaphore_wait(barrier, 7)


def fill_table(table, g_ref, o_ref, lse_ref, start_ref, pos_ref):
    heads, tokens = lse_ref.shape
    block = TILE * heads
    spread = (
        lax.broadcasted_iota(jnp.int32, (TILE, block), 1) // heads
        == lax.broadcasted_iota(jnp.int32, (TILE, block), 0)
    ).astype(jnp.bfloat16)
    choose = (
        lax.broadcasted_iota(jnp.int32, (heads, block), 1) % heads
        == lax.broadcasted_iota(jnp.int32, (heads, block), 0)
    )

    def spread_whole(values):
        upper = values // 256
        lower = values - upper * 256
        up, low = (
            jnp.dot(
                jnp.broadcast_to(part.astype(jnp.float32), (8, TILE)).astype(jnp.bfloat16),
                spread,
                preferred_element_type=jnp.float32,
            )
            for part in (upper, lower)
        )
        return (up * 256.0 + low)[0:1]

    ones = jnp.ones((8, g_ref.shape[1]), jnp.bfloat16)
    for c in range(g_ref.shape[0] // block):
        r = pl.ds(c * block, block)
        product = g_ref[r].astype(jnp.float32) * o_ref[r].astype(jnp.float32)
        upper = product.astype(jnp.bfloat16)
        lower = (product - upper.astype(jnp.float32)).astype(jnp.bfloat16)
        delta = lax.dot_general(
            ones, upper, ROWS, preferred_element_type=jnp.float32
        ) + lax.dot_general(ones, lower, ROWS, preferred_element_type=jnp.float32)
        table[0:1, r] = delta[0:1]
        rest = lse_ref[:, c * TILE : (c + 1) * TILE] * LOG2E
        lse = jnp.zeros((heads, block), jnp.float32)
        for _ in range(3):
            part = rest.astype(jnp.bfloat16)
            rest = rest - part.astype(jnp.float32)
            lse += jnp.dot(part, spread, preferred_element_type=jnp.float32)
        table[1:2, r] = jnp.sum(jnp.where(choose, lse, 0.0), axis=0, keepdims=True)
        at = slice(c * TILE, (c + 1) * TILE)
        table[2:3, r] = spread_whole(start_ref[:, at])
        table[3:4, r] = spread_whole(pos_ref[:, at])


def kernel(
    n, k_hbm, v_hbm, lse_hbm, start_hbm, pos_hbm, q_hbm, g_hbm, o_hbm,
    dq_ref, total, last,
    kv, q_ref, g_ref, o_ref, lse_ref, start_ref, pos_ref, marks, table,
    kp_buf, own_kp, p_buf, ds_buf, dk_acc, dv_acc, dq_acc,
    part, near, mid, guest, extra, send, recv, local,
):
    b, h, even, partner, at = places(n)
    _, tokens, double = kv.shape
    width = double // 2
    heads = lse_ref.shape[0]
    block = TILE * heads
    count = tokens // TILE
    chunks = tokens // CHUNK
    per = CHUNK // TILE
    scaling = width ** (-0.5)
    left, right = slice(0, width), slice(width, double)

    def copy(src, dst, kind, c, who):
        return pltpu.make_async_remote_copy(
            src_ref=src,
            dst_ref=dst,
            send_sem=send.at[kind, c],
            recv_sem=recv.at[kind, c],
            device_id=who,
            device_id_type=MESH,
        )

    loads = [
        pltpu.make_async_copy(src, dst, local.at[j])
        for j, (src, dst) in enumerate(
            (
                (k_hbm, kv.at[0, :, left]),
                (v_hbm, kv.at[0, :, right]),
                (pos_hbm, pos_ref),
                (g_hbm, g_ref),
                (o_hbm, o_ref),
                (lse_hbm, lse_ref),
                (start_hbm, start_ref),
                (q_hbm, q_ref),
            )
        )
    ]
    for c in loads:
        c.start()
    greet(n)

    first, other, fwd, give, own, hop, side = {}, {}, {}, {}, {}, {}, {}
    slot = jnp.where(even, 1, 3)
    flip = jnp.where(even, 3, 1)
    for c in range(chunks):
        r = pl.ds(c * CHUNK, CHUNK)
        first[c] = copy(kv.at[0, r], kv.at[2, r], 0, c, (at(-2), h))
        other[c] = copy(
            kv.at[0, r], kv.at[flip, r], 1, c, (jnp.where(even, at(-3), partner), h)
        )
        fwd[c] = copy(kv.at[2, r], kv.at[slot, r], 2, c, (partner, h))
        give[c] = copy(part.at[flip, r], near.at[r], 3, c, (partner, h))
        own[c] = copy(
            part.at[slot, r], extra.at[r], 4, c, (jnp.where(even, partner, at(3)), h)
        )
        hop[c] = copy(mid.at[r], guest.at[r], 5, c, (at(2), h))
        side[c] = copy(total.at[r], last.at[r], 6, c, (b, 1 - h))
    note = [
        copy(pos_ref.at[:, left], marks.at[d], 7, d, (at(-d), h)) for d in range(1, STEPS)
    ]

    for c in loads[:3]:
        c.wait()
    for c in note:
        c.start()
    for c in reversed(range(chunks)):
        first[c].start()
        other[c].start()

    dq_acc[...] = jnp.zeros_like(dq_acc)
    ramp = lax.broadcasted_iota(jnp.int32, (CHUNK, width), 0) * n
    own_kp[...] = (ramp + pos_ref[0:1, 0:1]).astype(jnp.float32)
    for c in loads[3:7]:
        c.wait()
    fill_table(table, g_ref, o_ref, lse_ref, start_ref, pos_ref)
    loads[7].wait()
    for c in note:
        c.wait()
    for s in range(1, STEPS):
        kp_buf[(s - 1) * TILE : s * TILE, :] = (
            ramp[:TILE] + marks[s, 0:1, 0:1]
        ).astype(jnp.float32)

    def lanes(i):
        if isinstance(i, int):
            return pl.ds(i * block, block)
        return pl.ds(pl.multiple_of(i * block, block), block)

    def keys_of(unit):
        kind, t = unit
        if kind == 0:
            rows = kv[1:STEPS, t * TILE : (t + 1) * TILE, :]
            return rows.reshape((STEPS - 1) * TILE, double), kp_buf, t * (TILE * n)
        return kv[0, t * CHUNK : (t + 1) * CHUNK, :], own_kp, t * (CHUNK * n)

    def probs(unit, i, causal):
        rows, places_of, moved = keys_of(unit)
        r = lanes(i)
        start = table[2:3, r] - float(moved)
        kp = jnp.concatenate([places_of[...]] * (block // width), axis=1)
        s = lax.dot_general(rows[:, left], q_ref[r, :], ROWS, preferred_element_type=jnp.float32)
        dp = lax.dot_general(rows[:, right], g_ref[r, :], ROWS, preferred_element_type=jnp.float32)
        ok = kp >= start
        if causal:
            ok = ok & (kp <= table[3:4, r] - float(moved))
        p = jnp.where(ok, jnp.exp2(s * (scaling * LOG2E) - table[1:2, r]), 0.0)
        return p.astype(jnp.bfloat16), (p * (dp - table[0:1, r])).astype(jnp.bfloat16)

    def put(pair):
        size = pair[0].shape[0]
        p_buf[:size], ds_buf[:size] = pair

    def add_grads(unit, i):
        rows, _, _ = keys_of(unit)
        size = rows.shape[0]
        r = lanes(i)
        ds = ds_buf[:size]
        dv_acc[:size] += jnp.dot(p_buf[:size], g_ref[r, :], preferred_element_type=jnp.float32)
        dk_acc[:size] += jnp.dot(ds, q_ref[r, :], preferred_element_type=jnp.float32)
        dq_acc[:, r] += lax.dot_general(
            rows[:, left], ds, COLS, preferred_element_type=jnp.float32
        )

    def clear():
        dk_acc[...] = jnp.zeros_like(dk_acc)
        dv_acc[...] = jnp.zeros_like(dv_acc)

    def arrive(c):
        other[c].wait_recv()
        fwd[c].wait_recv()

    def relay(c):
        first[c].wait_recv()
        fwd[c].start()

    def merge(c):
        r = pl.ds(c * CHUNK, CHUNK)
        give[c].wait_recv()
        mid[r] = (part[2, r].astype(jnp.float32) + near[r].astype(jnp.float32)).astype(mid.dtype)
        hop[c].start()

    units = [((0, t), t) for t in reversed(range(count))]
    units += [((1, c), c * per) for c in reversed(range(chunks))]

    def after(unit):
        kind, t = unit
        if kind == 0:
            at_rows = slice(t * TILE, (t + 1) * TILE)
            for s in range(1, STEPS):
                mine = slice((s - 1) * TILE, s * TILE)
                part[s, at_rows, left] = (dk_acc[mine] * scaling).astype(part.dtype)
                part[s, at_rows, right] = dv_acc[mine].astype(part.dtype)
            clear()
            c = t // per
            if t % per == 0:
                give[c].start()
                own[c].start()
            elif c + 1 < chunks:
                merge(c + 1)
        else:
            if t == chunks - 1:
                merge(0)
            r = pl.ds(t * CHUNK, CHUNK)
            hop[t].wait_recv()
            own[t].wait_recv()
            both = guest[r].astype(jnp.float32) + extra[r].astype(jnp.float32)
            total[r, left] = (dk_acc[:CHUNK] * scaling + both[:, left]).astype(total.dtype)
            total[r, right] = (dv_acc[:CHUNK] + both[:, right]).astype(total.dtype)
            clear()
            side[t].start()

    clear()
    relay(chunks - 1)
    arrive(chunks - 1)
    put(probs(*units[0], True))
    for j, (unit, low) in enumerate(units):
        kind, t = unit

        def body(i, carry, unit=unit, kind=kind):
            pair = probs(unit, i, kind == 1)
            add_grads(unit, i - 1)
            put(pair)
            return carry

        if low + 1 < count:
            lax.fori_loop(low + 1, count, body, 0)
        if kind == 0 and t > 0:
            if t % per == 0:
                arrive(t // per - 1)
            elif t // per > 0:
                relay(t // per - 1)
        if j + 1 < len(units):
            pair = probs(*units[j + 1], True)
            add_grads(unit, count - 1)
            put(pair)
        else:
            add_grads(unit, count - 1)
        after(unit)

    for i in range(count):
        r = lanes(i)
        dq_ref[r, :] = (dq_acc[:, r].T * scaling).astype(dq_ref.dtype)
    for c in range(chunks):
        for x in (first[c], other[c], fwd[c], give[c], own[c], hop[c]):
            x.wait_send()
        side[c].wait()


def fused(n, k, v, lse, start, pos, q, g, o):
    rows, width = k.shape
    heads = lse.shape[0]
    block = TILE * heads
    keys = max((STEPS - 1) * TILE, CHUNK)
    chunks = rows // CHUNK
    pair = (rows, 2 * width)
    low = jnp.bfloat16
    f32 = jnp.float32
    return pl.pallas_call(
        functools.partial(kernel, n),
        out_shape=(
            jax.ShapeDtypeStruct(q.shape, q.dtype),
            jax.ShapeDtypeStruct(pair, low),
            jax.ShapeDtypeStruct(pair, low),
        ),
        in_specs=[ANY_SPEC] * 8,
        out_specs=(VMEM_SPEC,) * 3,
        scratch_shapes=[
            pltpu.VMEM((STEPS,) + pair, low),
            pltpu.VMEM(q.shape, low),
            pltpu.VMEM(q.shape, low),
            pltpu.VMEM(q.shape, low),
            pltpu.VMEM(lse.shape, f32),
            pltpu.VMEM(start.shape, start.dtype),
            pltpu.VMEM(pos.shape, pos.dtype),
            pltpu.VMEM((STEPS, 1, width), pos.dtype),
            pltpu.VMEM((4, q.shape[0]), f32),
            pltpu.VMEM(((STEPS - 1) * TILE, width), f32),
            pltpu.VMEM((CHUNK, width), f32),
            pltpu.VMEM((keys, block), low),
            pltpu.VMEM((keys, block), low),
            pltpu.VMEM((keys, width), f32),
            pltpu.VMEM((keys, width), f32),
            pltpu.VMEM((width, q.shape[0]), f32),
            pltpu.VMEM((STEPS,) + pair, low),
            pltpu.VMEM(pair, low),
            pltpu.VMEM(pair, low),
            pltpu.VMEM(pair, low),
            pltpu.VMEM(pair, low),
            pltpu.SemaphoreType.DMA((8, max(chunks, STEPS))),
            pltpu.SemaphoreType.DMA((8, max(chunks, STEPS))),
            pltpu.SemaphoreType.DMA((8,)),
        ],
        compiler_params=pltpu.CompilerParams(
            collective_id=0, has_side_effects=True, vmem_limit_bytes=60 << 20
        ),
        name="fused_grads",
    )(k, v, lse, start, pos, q, g, o)


def on_device(
    n, queries, out_grad, outputs, key_vectors, value_vectors, logsumexp, positions, doc_start
):
    width = queries.shape[-1]
    flat = (-1, width)
    dq, total, last = fused(
        n, key_vectors, value_vectors, logsumexp.T, doc_start.reshape(1, -1),
        positions.reshape(1, -1), queries.reshape(flat), out_grad.reshape(flat),
        outputs.reshape(flat),
    )
    both = (total.astype(jnp.float32) + last.astype(jnp.float32)).astype(jnp.bfloat16)
    return dq.reshape(queries.shape), both[:, :width], both[:, width:]


def solution(mesh):
    n = mesh.shape["blk"]
    in_specs = (
        P("blk", "head", None),
        P("blk", "head", None),
        P("blk", "head", None),
        P("blk", None),
        P("blk", None),
        P("blk", "head"),
        P("blk"),
        P("blk"),
    )
    out_specs = (P("blk", "head", None), P("blk", None), P("blk", None))
    return jax.shard_map(
        functools.partial(on_device, n),
        mesh=mesh,
        in_specs=in_specs,
        out_specs=out_specs,
        check_vma=False,
    )
```

time: 55.6 us -> 44.9 us (0.81)
  Pallas kernels: 48.1 us -> 41.2 us
  local copies, waits for them, and re-layouts: 5.66 us -> 1.69 us
    pallas_call x3 -> x1, Pallas kernels: 48.1 us -> 41.2 us  [fused(): pl.pallas_call(functools.partial(kernel, n), out_shape=(jax.ShapeDtypeStr...]
    unnamed x18 -> x3, local copies, waits for them, and re-layouts: 5.66 us -> 0.97 us
    slice x0 -> x1, local copies, waits for them, and re-layouts: none -> 0.72 us  [on_device(): return (dq.reshape(queries.shape), both[:, :width], both[:, width:])]
where the time goes in v1:
time: 44.9 us; the launch traced here: 44.8 us
  Pallas kernels  41.2 us (92%)
  local copies, waits for them, and re-layouts  1.69 us (4%)
  other arithmetic  1.18 us (3%)
  between operations  0.65 us (1%)
    pallas_call x1, Pallas kernels, fused(): pl.pallas_call(functools.partial(kernel, n), out_shape=(jax.ShapeDtypeStr...  41.2 us
    convert_element_type x1, other arithmetic, on_device(): (total.astype(jnp.float32) + last.astype(jnp.float32)).astype(jnp.bfloat16)  1.18 us
    unnamed x3, local copies, waits for them, and re-layouts  0.97 us

profile of v1, /device:TPU:0, one launch (start us, length us, event | category | flops | bytes accessed | tf_op | source)
XLA Modules:
  0.0 44.8 jit_solution(11490976597343008138)
XLA Ops:
  0.6 41.2 %fused_grads.1 = (bf16[4096,128]{1,0:T(8,128)(2,1)}, bf16[512,256]{1,0:T(8,128)(2,1)}, bf16[512,256]{1,0:T(8,128)(2,1)}) custom-call(bf16[512,128]{1,0:T(8,128)(2,1)} %k_hbm.1, bf16[512,128]{1,0:T(8,128)(2,1)} %v_hbm.1, f32[8,512]{1,0:T(8,128)} %bitcast.11, s32[1,512]{1,0:T(1,128)} %bitcast.12, s32[1,512]{1,0:T(1,128)} %bitcast.13, ...), custom_call_target="tpu_custom_call" | custom-call | tf_op jit(solution)/shard_map/fused_grads/pallas_call | solution.py:313
  41.9 0.0 copy-start
  41.9 1.2 %add_convert_fusion = bf16[512,256]{1,0:T(8,128)(2,1)S(1)} fusion(bf16[512,256]{1,0:T(8,128)(2,1)} %get-tuple-element.8, bf16[512,256]{1,0:T(8,128)(2,1)} %get-tuple-element.7), kind=kLoop, calls=%fused_computation | loop fusion | flops 524288 | bytes 786432 | tf_op jit(solution)/shard_map/convert_element_type | solution.py:365
  43.1 0.7 %fusion = (bf16[512,128]{1,0:T(8,128)(2,1)}, bf16[512,128]{1,0:T(8,128)(2,1)}) fusion(bf16[512,256]{1,0:T(8,128)(2,1)S(1)} %add_convert_fusion), kind=kLoop, calls=%fused_computation.1 | loop fusion | bytes 524288 | tf_op jit(solution)/shard_map/slice | solution.py:366
  43.8 0.0 copy-done
  43.8 1.0 %copy.12 = bf16[512,8,128]{2,1,0:T(8,128)(2,1)} copy(bf16[512,8,128]{2,1,0:T(8,128)(2,1)S(1)} %bitcast.7) | data formatting | bytes 2097152
Async XLA Ops:
  41.9 1.9 %copy-start = (bf16[4096,128]{1,0:T(8,128)(2,1)S(1)}, bf16[4096,128]{1,0:T(8,128)(2,1)}, u32[]{:S(2)}) copy-start(bf16[4096,128]{1,0:T(8,128)(2,1)} %get-tuple-element.6) | copy-start | bytes 3145732

commit v2 on v1

v2 whole, which is shorter than its diff:
```python
import functools
import math

import jax
import jax.numpy as jnp
from jax import lax
from jax.experimental import pallas as pl
from jax.experimental.pallas import tpu as pltpu
from jax.sharding import PartitionSpec as P

STEPS = 4
TILE = 64
CHUNK = 128
MERGED = 2
LOG2E = math.log2(math.e)
MESH = pl.DeviceIdType.MESH
VMEM_SPEC = pl.BlockSpec(memory_space=pltpu.VMEM)
ANY_SPEC = pl.BlockSpec(memory_space=pl.ANY)
ROWS = (((1,), (1,)), ((), ()))
COLS = (((0,), (0,)), ((), ()))


def places(n):
    b = lax.axis_index("blk")
    h = lax.axis_index("head")
    even = lax.rem(b, 2) == 0
    partner = jnp.where(even, b + 1, b - 1)

    def at(d):
        return lax.rem(b + d + n, n)

    return b, h, even, partner, at


def greet(n):
    b, h, even, partner, at = places(n)
    barrier = pltpu.get_barrier_semaphore()
    for d in (-3, -2, -1, 1, 2, 3):
        for p in (h, 1 - h):
            pl.semaphore_signal(barrier, inc=1, device_id=(at(d), p), device_id_type=MESH)
    pl.semaphore_signal(barrier, inc=1, device_id=(b, 1 - h), device_id_type=MESH)
    pl.semaphore_wait(barrier, 13)


def fill_table(table, g_ref, o_ref, lse_ref, start_ref, pos_ref):
    heads, tokens = lse_ref.shape
    block = TILE * heads
    spread = (
        lax.broadcasted_iota(jnp.int32, (TILE, block), 1) // heads
        == lax.broadcasted_iota(jnp.int32, (TILE, block), 0)
    ).astype(jnp.bfloat16)
    choose = (
        lax.broadcasted_iota(jnp.int32, (heads, block), 1) % heads
        == lax.broadcasted_iota(jnp.int32, (heads, block), 0)
    )

    def spread_whole(values):
        upper = values // 256
        lower = values - upper * 256
        up, low = (
            jnp.dot(
                jnp.broadcast_to(part.astype(jnp.float32), (8, TILE)).astype(jnp.bfloat16),
                spread,
                preferred_element_type=jnp.float32,
            )
            for part in (upper, lower)
        )
        return (up * 256.0 + low)[0:1]

    ones = jnp.ones((8, g_ref.shape[1]), jnp.bfloat16)
    for c in range(g_ref.shape[0] // block):
        r = pl.ds(c * block, block)
        product = g_ref[r].astype(jnp.float32) * o_ref[r].astype(jnp.float32)
        upper = product.astype(jnp.bfloat16)
        lower = (product - upper.astype(jnp.float32)).astype(jnp.bfloat16)
        delta = lax.dot_general(
            ones, upper, ROWS, preferred_element_type=jnp.float32
        ) + lax.dot_general(ones, lower, ROWS, preferred_element_type=jnp.float32)
        table[0:1, r] = delta[0:1]
        rest = lse_ref[:, c * TILE : (c + 1) * TILE] * LOG2E
        lse = jnp.zeros((heads, block), jnp.float32)
        for _ in range(3):
            part = rest.astype(jnp.bfloat16)
            rest = rest - part.astype(jnp.float32)
            lse += jnp.dot(part, spread, preferred_element_type=jnp.float32)
        table[1:2, r] = jnp.sum(jnp.where(choose, lse, 0.0), axis=0, keepdims=True)
        at = slice(c * TILE, (c + 1) * TILE)
        table[2:3, r] = spread_whole(start_ref[:, at])
        table[3:4, r] = spread_whole(pos_ref[:, at])


def kernel(
    n, k_hbm, v_hbm, lse_hbm, start_hbm, pos_hbm, q_hbm, g_hbm, o_hbm,
    dq_ref, out_ref,
    kv, q_ref, g_ref, o_ref, lse_ref, start_ref, pos_ref, marks, table,
    kp_buf, own_kp, p_buf, ds_buf, dk_acc, dv_acc, dq_acc,
    part, mine, near, mid, total, last, sums, box, send, recv, local,
):
    b, h, even, partner, at = places(n)
    _, tokens, double = kv.shape
    width = double // 2
    heads = lse_ref.shape[0]
    block = TILE * heads
    count = tokens // TILE
    chunks = tokens // CHUNK
    per = CHUNK // TILE
    scaling = width ** (-0.5)
    left, right = slice(0, width), slice(width, double)
    groups, segs = segments(count)

    def copy(src, dst, out, into, who):
        return pltpu.make_async_remote_copy(
            src_ref=src,
            dst_ref=dst,
            send_sem=send.at[out],
            recv_sem=recv.at[into],
            device_id=who,
            device_id_type=MESH,
        )

    loads = [
        pltpu.make_async_copy(src, dst, local.at[j])
        for j, (src, dst) in enumerate(
            (
                (k_hbm, kv.at[0, :, left]),
                (v_hbm, kv.at[0, :, right]),
                (pos_hbm, pos_ref),
                (g_hbm, g_ref),
                (o_hbm, o_ref),
                (lse_hbm, lse_ref),
                (start_hbm, start_ref),
                (q_hbm, q_ref),
            )
        )
    ]
    for c in loads:
        c.start()
    greet(n)

    slot = jnp.where(even, 1, 3)
    flip = jnp.where(even, 3, 1)
    group_rows, rows_of = (
        [pl.ds(seg[-1] * TILE, len(seg) * TILE) for seg in split] for split in (groups, segs)
    )
    first, other, fwd, give, own, hop, side, straight = ([] for _ in range(8))
    arrived, summed = [], []
    me = (b, h)
    tail = len(segs) - 1
    kinds = (len(groups), len(groups), MERGED, MERGED, len(segs), len(segs), 1)
    base = [sum(kinds[:j]) for j in range(len(kinds))]
    for c, r in enumerate(group_rows):
        first.append(copy(kv.at[0, r], kv.at[2, r], 0, base[0] + c, (at(-2), h)))
        to = (jnp.where(even, at(-3), partner), h)
        other.append(copy(kv.at[0, r], kv.at[flip, r], 1, base[1] + c, to))
        fwd.append(copy(kv.at[2, r], kv.at[slot, r], 2, base[1] + c, (partner, h)))
        arrived.append(copy(kv.at[0:2, r], kv.at[0:2, r], 0, base[1] + c, me))
    for c, r in enumerate(rows_of):
        side.append(copy(total.at[r], last.at[r], 6, base[4] + c, (b, 1 - h)))
        if c >= MERGED:
            planes = (h, 1 - h) if c == tail else (h,)
            straight.append(
                [
                    copy(part.at[s, r], box.at[p, s, r], 8 + p, base[5] + c, (at(s), who))
                    for p, who in enumerate(planes)
                    for s in range(1, STEPS)
                ]
            )
            whole = box.at[0 : len(planes), 1:STEPS, r]
            summed.append(copy(whole, whole, 0, base[5] + c, me))
            continue
        give.append(copy(part.at[flip, r], near.at[r], 3, base[2] + c, (partner, h)))
        to = (jnp.where(even, partner, at(3)), h)
        own.append(copy(part.at[slot, r], sums.at[0, r], 4, base[3] + c, to))
        hop.append(copy(mid.at[r], sums.at[1, r], 5, base[3] + c, (at(2), h)))
        summed.append(copy(sums.at[:, r], sums.at[:, r], 0, base[3] + c, me))
    note = [
        copy(pos_ref.at[:, left], marks.at[d], 7, base[6], (at(-d), h))
        for d in range(1, STEPS)
    ]
    noted = copy(marks.at[1:STEPS], marks.at[1:STEPS], 7, base[6], me)
    merged = pl.ds(segs[MERGED - 1][-1] * TILE, tokens - segs[MERGED - 1][-1] * TILE)
    rest = pl.ds(0, segs[MERGED - 1][-1] * TILE)
    sent = [copy(kv.at[0], kv.at[2], j, 0, me) for j in range(3)]
    sent += [copy(mid.at[merged], near.at[merged], j, 0, me) for j in range(3, 6)]
    sent += [copy(total, last, 6, 0, me), noted]
    sent.append(copy(part.at[1:STEPS, rest], box.at[0, 1:STEPS, rest], 8, 0, me))
    final = rows_of[tail]
    sent.append(copy(part.at[1:STEPS, final], box.at[1, 1:STEPS, final], 9, 0, me))

    for c in loads[:3]:
        c.wait()
    for c in note:
        c.start()
    for x, y in zip(first, other):
        x.start()
        y.start()

    ramp = lax.broadcasted_iota(jnp.int32, (CHUNK, width), 0) * n
    own_kp[...] = (ramp + pos_ref[0:1, 0:1]).astype(jnp.float32)
    for c in loads[3:7]:
        c.wait()
    fill_table(table, g_ref, o_ref, lse_ref, start_ref, pos_ref)
    loads[7].wait()

    def lanes(i):
        return pl.ds(i * block, block)

    def keys_of(unit):
        kind, t = unit
        if kind == 1:
            rows = kv[1:STEPS, t * TILE : (t + 1) * TILE, :]
            return rows.reshape((STEPS - 1) * TILE, double), kp_buf, t * (TILE * n)
        return kv[0, t * CHUNK : (t + 1) * CHUNK, :], own_kp, t * (CHUNK * n)

    def probs(unit, i):
        kind, t = unit
        causal = i < (t + 1) * (per if kind == 0 else 1)
        rows, places_of, moved = keys_of(unit)
        r = lanes(i)
        start = table[2:3, r] - float(moved)
        kp = jnp.concatenate([places_of[...]] * (block // width), axis=1)
        s = lax.dot_general(rows[:, left], q_ref[r, :], ROWS, preferred_element_type=jnp.float32)
        dp = lax.dot_general(rows[:, right], g_ref[r, :], ROWS, preferred_element_type=jnp.float32)
        ok = kp >= start
        if causal:
            ok = ok & (kp <= table[3:4, r] - float(moved))
        p = jnp.where(ok, jnp.exp2(s * (scaling * LOG2E) - table[1:2, r]), 0.0)
        return p.astype(jnp.bfloat16), (p * (dp - table[0:1, r])).astype(jnp.bfloat16)

    def put(pair, turn):
        size = pair[0].shape[0]
        p_buf[turn, :size], ds_buf[turn, :size] = pair

    seen = set()

    def add(ref, index, value, fresh):
        ref[index] = value if fresh else ref[index] + value

    def add_grads(unit, i, turn, fresh):
        rows, _, _ = keys_of(unit)
        size = rows.shape[0]
        r = lanes(i)
        ds = ds_buf[turn, :size]
        dv = jnp.dot(p_buf[turn, :size], g_ref[r, :], preferred_element_type=jnp.float32)
        dk = jnp.dot(ds, q_ref[r, :], preferred_element_type=jnp.float32)
        dq = lax.dot_general(rows[:, left], ds, COLS, preferred_element_type=jnp.float32)
        add(dv_acc, slice(0, size), dv, fresh)
        add(dk_acc, slice(0, size), dk, fresh)
        add(dq_acc, (slice(None), r), dq, i not in seen)
        seen.add(i)

    def arrive(c):
        arrived[c].wait_recv()

    def relay(c):
        first[c].wait_recv()
        fwd[c].start()

    def merge(c):
        r = rows_of[c]
        give[c].wait_recv()
        mid[r] = (part[2, r].astype(jnp.float32) + near[r].astype(jnp.float32)).astype(mid.dtype)
        hop[c].start()

    def settle(c):
        r = rows_of[c]
        if c >= MERGED:
            summed[c].wait_recv()
            near_sum = sum(box[0, s, r].astype(jnp.float32) for s in range(1, STEPS))
            if c == tail:
                far_sum = sum(box[1, s, r].astype(jnp.float32) for s in range(1, STEPS))
                side[c].wait_recv()
                a = total[r].astype(jnp.float32) + near_sum
                out_ref[r] = (a + (last[r].astype(jnp.float32) + far_sum)).astype(out_ref.dtype)
            else:
                total[r] = (mine[r] + near_sum).astype(total.dtype)
                side[c].start()
            return
        summed[c].wait_recv()
        both = sums[1, r].astype(jnp.float32) + sums[0, r].astype(jnp.float32)
        total[r] = (mine[r] + both).astype(total.dtype)
        side[c].start()

    def finish(unit):
        kind, t = unit
        if kind == 0:
            r = pl.ds(t * CHUNK, CHUNK)
            mine[r, left] = dk_acc[:CHUNK] * scaling
            mine[r, right] = dv_acc[:CHUNK]
        else:
            at_rows = slice(t * TILE, (t + 1) * TILE)
            for s in range(1, STEPS):
                rows = slice((s - 1) * TILE, s * TILE)
                part[s, at_rows, left] = (dk_acc[rows] * scaling).astype(part.dtype)
                part[s, at_rows, right] = dv_acc[rows].astype(part.dtype)

    work, acts, ends = [], {}, {}
    for t in reversed(range(chunks)):
        work += [((0, t), i) for i in range(t * per, count)]
    acts[len(work) - 1 - count // 2] = [("relay", 0)]
    acts[len(work) - 1] = [("note", 0), ("relay", 1), ("arrive", 0)]
    begins = {}
    for t in reversed(range(count)):
        begins[t] = len(work)
        work += [((1, t), i) for i in range(t, count)]
        for c, seg in enumerate(segs):
            if seg[-1] == t:
                ends[len(work) - 1] = c
    for c in range(1, len(groups)):
        todo = acts.setdefault(begins[groups[c][0]] - 1, [])
        if c + 1 < len(groups):
            todo.append(("relay", c + 1))
        todo.append(("arrive", c))
        if c == 1:
            todo.append(("mine", tail))
    def act(name, c):
        if name == "note":
            noted.wait_recv()
            for s in range(1, STEPS):
                kp_buf[(s - 1) * TILE : s * TILE, :] = (
                    ramp[:TILE] + marks[s, 0:1, 0:1]
                ).astype(jnp.float32)
        elif name == "mine":
            r = rows_of[c]
            total[r] = mine[r].astype(total.dtype)
            side[c].start()
        elif name == "relay":
            relay(c)
        elif name == "arrive":
            arrive(c)
        else:
            merge(c)

    put(probs(*work[0]), 0)
    for j, (unit, i) in enumerate(work):
        for name, c in acts.get(j, []):
            act(name, c)
        if j + 1 < len(work):
            put(probs(*work[j + 1]), (j + 1) % 2)
        add_grads(unit, i, j % 2, j == 0 or work[j - 1][0] != unit)
        if j + 1 == len(work) or work[j + 1][0] != unit:
            finish(unit)
        if j in ends:
            c = ends[j]
            if c < MERGED:
                give[c].start()
                own[c].start()
            else:
                for x in straight[c - MERGED]:
                    x.start()
            if 0 < c <= MERGED:
                merge(c - 1)

    def write(i):
        r = lanes(i)
        dq_ref[r, :] = (dq_acc[:, r].T * scaling).astype(dq_ref.dtype)

    for i in range(count):
        write(i)
    for c in range(tail + 1):
        settle(c)
    for c, r in enumerate(rows_of[:tail]):
        side[c].wait_recv()
        out_ref[r] = (total[r].astype(jnp.float32) + last[r].astype(jnp.float32)).astype(out_ref.dtype)
    for x in sent:
        x.wait_send()


def segments(count):
    tiles = list(reversed(range(count)))
    arriving = [tiles[:2]] + [[t] for t in tiles[2:-2]] + [tiles[-2:]]
    leaving = [tiles[: count - 5], tiles[count - 5 : count - 3]]
    leaving += [[t] for t in tiles[count - 3 :]]
    return arriving, leaving


def fused(n, k, v, lse, start, pos, q, g, o):
    rows, width = k.shape
    heads = lse.shape[0]
    block = TILE * heads
    keys = max((STEPS - 1) * TILE, CHUNK)
    pair = (rows, 2 * width)
    low = jnp.bfloat16
    f32 = jnp.float32
    groups, segs = segments(rows // TILE)
    landings = 2 * len(groups) + 2 * MERGED + 2 * len(segs) + 1
    k, v, lse, start, pos, q, g, o = (
        pltpu.with_memory_space_constraint(x, pltpu.HBM)
        for x in (k, v, lse, start, pos, q, g, o)
    )
    return pl.pallas_call(
        functools.partial(kernel, n),
        out_shape=(
            jax.ShapeDtypeStruct(q.shape, q.dtype),
            jax.ShapeDtypeStruct(pair, low),
        ),
        in_specs=[ANY_SPEC] * 8,
        out_specs=(VMEM_SPEC, VMEM_SPEC),
        scratch_shapes=[
            pltpu.VMEM((STEPS,) + pair, low),
            pltpu.VMEM(q.shape, low),
            pltpu.VMEM(q.shape, low),
            pltpu.VMEM(q.shape, low),
            pltpu.VMEM(lse.shape, f32),
            pltpu.VMEM(start.shape, start.dtype),
            pltpu.VMEM(pos.shape, pos.dtype),
            pltpu.VMEM((STEPS, 1, width), pos.dtype),
            pltpu.VMEM((4, q.shape[0]), f32),
            pltpu.VMEM(((STEPS - 1) * TILE, width), f32),
            pltpu.VMEM((CHUNK, width), f32),
            pltpu.VMEM((2, keys, block), low),
            pltpu.VMEM((2, keys, block), low),
            pltpu.VMEM((keys, width), f32),
            pltpu.VMEM((keys, width), f32),
            pltpu.VMEM((width, q.shape[0]), f32),
            pltpu.VMEM((STEPS,) + pair, low),
            pltpu.VMEM(pair, f32),
        ]
        + [pltpu.VMEM(pair, low)] * 4
        + [pltpu.VMEM((2,) + pair, low), pltpu.VMEM((2, STEPS) + pair, low)]
        + [pltpu.SemaphoreType.DMA((count,)) for count in (10, landings, 8)],
        compiler_params=pltpu.CompilerParams(
            collective_id=0, has_side_effects=True, vmem_limit_bytes=32 << 20
        ),
        name="fused_grads",
    )(k, v, lse, start, pos, q, g, o)


def on_device(
    n, queries, out_grad, outputs, key_vectors, value_vectors, logsumexp, positions, doc_start
):
    width = queries.shape[-1]
    flat = (-1, width)
    dq, both = fused(
        n, key_vectors, value_vectors, logsumexp.T, doc_start.reshape(1, -1),
        positions.reshape(1, -1), queries.reshape(flat), out_grad.reshape(flat),
        outputs.reshape(flat),
    )
    return dq.reshape(queries.shape), both[:, :width], both[:, width:]


def solution(mesh):
    n = mesh.shape["blk"]
    in_specs = (
        P("blk", "head", None),
        P("blk", "head", None),
        P("blk", "head", None),
        P("blk", None),
        P("blk", None),
        P("blk", "head"),
        P("blk"),
        P("blk"),
    )
    out_specs = (P("blk", "head", None), P("blk", None), P("blk", None))
    return jax.shard_map(
        functools.partial(on_device, n),
        mesh=mesh,
        in_specs=in_specs,
        out_specs=out_specs,
        check_vma=False,
    )
```

time: 44.9 us -> 37 us (0.82)
  Pallas kernels: 41.2 us -> 34.5 us
  other arithmetic: 1.18 us -> 0 us
    pallas_call x1, Pallas kernels: 41.2 us -> 34.5 us  [fused(): pl.pallas_call(functools.partial(kernel, n), out_shape=(jax.ShapeDtypeStr...]
    convert_element_type x1 -> x0, other arithmetic: 1.18 us -> none  [on_device(): (total.astype(jnp.float32) + last.astype(jnp.float32)).astype(jnp.bfloat16)]
    unnamed x3 -> x1, local copies, waits for them, and re-layouts: 0.97 us -> 0.97 us
where the time goes in v2:
time: 37 us; the launch traced here: 36.9 us
  Pallas kernels  34.5 us (93%)
  local copies, waits for them, and re-layouts  1.69 us (5%)
  between operations  0.64 us (2%)
    pallas_call x1, Pallas kernels, fused(): pl.pallas_call(functools.partial(kernel, n), out_shape=(jax.ShapeDtypeStr...  34.5 us
    unnamed x1, local copies, waits for them, and re-layouts  0.97 us

profile of v2, /device:TPU:0, one launch (start us, length us, event | category | flops | bytes accessed | tf_op | source)
XLA Modules:
  0.0 36.9 jit_solution(10642081618462224128)
XLA Ops:
  0.6 34.5 %fused_grads.1 = (bf16[4096,128]{1,0:T(8,128)(2,1)S(1)}, bf16[512,256]{1,0:T(8,128)(2,1)S(1)}) custom-call(bf16[512,128]{1,0:T(8,128)(2,1)} %k_hbm.1, bf16[512,128]{1,0:T(8,128)(2,1)} %v_hbm.1, f32[8,512]{1,0:T(8,128)} %bitcast.11, s32[1,512]{1,0:T(1,128)} %bitcast.12, s32[1,512]{1,0:T(1,128)} %bitcast.13, bf16[4096,128]{1,0:T(8,128)(2,1)} %bitcast.8, ...), custom_call_target="tpu_custom_call" | custom-call | tf_op jit(solution)/shard_map/fused_grads/pallas_call | solution.py:391
  35.2 0.7 %fusion = (bf16[512,128]{1,0:T(8,128)(2,1)}, bf16[512,128]{1,0:T(8,128)(2,1)}) fusion(bf16[512,256]{1,0:T(8,128)(2,1)S(1)} %get-tuple-element.6), kind=kLoop, calls=%fused_computation | loop fusion | bytes 524288 | tf_op jit(solution)/shard_map/slice | solution.py:439
  35.9 1.0 %copy.12 = bf16[512,8,128]{2,1,0:T(8,128)(2,1)} copy(bf16[512,8,128]{2,1,0:T(8,128)(2,1)S(1)} %bitcast.7) | data formatting | bytes 2097152

commit v3 on v2

--- a/solution.py
+++ b/solution.py
@@ -91,7 +91,7 @@
 
 def kernel(
     n, k_hbm, v_hbm, lse_hbm, start_hbm, pos_hbm, q_hbm, g_hbm, o_hbm,
-    dq_ref, out_ref,
+    dq_ref, dk_ref, dv_ref,
     kv, q_ref, g_ref, o_ref, lse_ref, start_ref, pos_ref, marks, table,
     kp_buf, own_kp, p_buf, ds_buf, dk_acc, dv_acc, dq_acc,
     part, mine, near, mid, total, last, sums, box, send, recv, local,
@@ -191,9 +191,11 @@
         c.wait()
     for c in note:
         c.start()
-    for x, y in zip(first, other):
+    first[0].start()
+    for x, y in zip(first[1:], other):
         x.start()
         y.start()
+    other[-1].start()
 
     ramp = lax.broadcasted_iota(jnp.int32, (CHUNK, width), 0) * n
     own_kp[...] = (ramp + pos_ref[0:1, 0:1]).astype(jnp.float32)
@@ -212,42 +214,77 @@
             return rows.reshape((STEPS - 1) * TILE, double), kp_buf, t * (TILE * n)
         return kv[0, t * CHUNK : (t + 1) * CHUNK, :], own_kp, t * (CHUNK * n)
 
+    def parts_of(unit, i):
+        kind, t = unit
+        rows, places_of, _ = keys_of(unit)
+        if kind == 0 or i > t:
+            return [(rows, places_of[...], 0, block)]
+        half = TILE // 2
+        few = kv[1:STEPS, t * TILE : t * TILE + half, :].reshape((STEPS - 1) * half, double)
+        near_places = places_of[...].reshape(STEPS - 1, TILE, width)[:, :half]
+        near_places = near_places.reshape((STEPS - 1) * half, width)
+        mid_lane = block // 2
+        return [(rows, places_of[...], mid_lane, block), (few, near_places, 0, mid_lane)]
+
     def probs(unit, i):
         kind, t = unit
         causal = i < (t + 1) * (per if kind == 0 else 1)
-        rows, places_of, moved = keys_of(unit)
-        r = lanes(i)
-        start = table[2:3, r] - float(moved)
-        kp = jnp.concatenate([places_of[...]] * (block // width), axis=1)
-        s = lax.dot_general(rows[:, left], q_ref[r, :], ROWS, preferred_element_type=jnp.float32)
-        dp = lax.dot_general(rows[:, right], g_ref[r, :], ROWS, preferred_element_type=jnp.float32)
-        ok = kp >= start
-        if causal:
-            ok = ok & (kp <= table[3:4, r] - float(moved))
-        p = jnp.where(ok, jnp.exp2(s * (scaling * LOG2E) - table[1:2, r]), 0.0)
-        return p.astype(jnp.bfloat16), (p * (dp - table[0:1, r])).astype(jnp.bfloat16)
-
-    def put(pair, turn):
-        size = pair[0].shape[0]
-        p_buf[turn, :size], ds_buf[turn, :size] = pair
+        moved = keys_of(unit)[2]
+        done = []
+        for rows, kp, low_lane, high_lane in parts_of(unit, i):
+            r = pl.ds(i * block + low_lane, high_lane - low_lane)
+            start = table[2:3, r] - float(moved)
+            kp = jnp.concatenate([kp] * ((high_lane - low_lane) // width), axis=1)
+            s = lax.dot_general(
+                rows[:, left], q_ref[r, :], ROWS, preferred_element_type=jnp.float32
+            )
+            dp = lax.dot_general(
+                rows[:, right], g_ref[r, :], ROWS, preferred_element_type=jnp.float32
+            )
+            ok = kp >= start
+            if causal:
+                ok = ok & (kp <= table[3:4, r] - float(moved))
+            p = jnp.where(ok, jnp.exp2(s * (scaling * LOG2E) - table[1:2, r]), 0.0)
+            ds = p * (dp - table[0:1, r])
+            done.append((slice(low_lane, high_lane), p.astype(jnp.bfloat16), ds.astype(jnp.bfloat16)))
+        return done
+
+    def put(done, turn):
+        for at_lanes, p, ds in done:
+            p_buf[turn, : p.shape[0], at_lanes] = p
+            ds_buf[turn, : ds.shape[0], at_lanes] = ds
 
     seen = set()
 
     def add(ref, index, value, fresh):
         ref[index] = value if fresh else ref[index] + value
 
+    def spread_rows(many, few):
+        many = many.reshape(STEPS - 1, TILE, width)
+        few = few.reshape(STEPS - 1, TILE // 2, width)
+        top = many[:, : TILE // 2] + few
+        whole = jnp.concatenate([top, many[:, TILE // 2 :]], axis=1)
+        return whole.reshape((STEPS - 1) * TILE, width)
+
     def add_grads(unit, i, turn, fresh):
-        rows, _, _ = keys_of(unit)
-        size = rows.shape[0]
-        r = lanes(i)
-        ds = ds_buf[turn, :size]
-        dv = jnp.dot(p_buf[turn, :size], g_ref[r, :], preferred_element_type=jnp.float32)
-        dk = jnp.dot(ds, q_ref[r, :], preferred_element_type=jnp.float32)
-        dq = lax.dot_general(rows[:, left], ds, COLS, preferred_element_type=jnp.float32)
+        sums = []
+        for rows, _, low_lane, high_lane in parts_of(unit, i):
+            size = rows.shape[0]
+            r = pl.ds(i * block + low_lane, high_lane - low_lane)
+            p = p_buf[turn, :size, low_lane:high_lane]
+            ds = ds_buf[turn, :size, low_lane:high_lane]
+            dv = jnp.dot(p, g_ref[r, :], preferred_element_type=jnp.float32)
+            dk = jnp.dot(ds, q_ref[r, :], preferred_element_type=jnp.float32)
+            dq = lax.dot_general(rows[:, left], ds, COLS, preferred_element_type=jnp.float32)
+            add(dq_acc, (slice(None), r), dq, i not in seen)
+            sums.append((dv, dk))
+        seen.add(i)
+        dv, dk = sums[0]
+        if len(sums) > 1:
+            dv, dk = (spread_rows(x, y) for x, y in zip(*sums))
+        size = dv.shape[0]
         add(dv_acc, slice(0, size), dv, fresh)
         add(dk_acc, slice(0, size), dk, fresh)
-        add(dq_acc, (slice(None), r), dq, i not in seen)
-        seen.add(i)
 
     def arrive(c):
         arrived[c].wait_recv()
@@ -261,6 +298,10 @@
         give[c].wait_recv()
         mid[r] = (part[2, r].astype(jnp.float32) + near[r].astype(jnp.float32)).astype(mid.dtype)
         hop[c].start()
+
+    def release(r, both):
+        dk_ref[r] = both[:, left].astype(dk_ref.dtype)
+        dv_ref[r] = both[:, right].astype(dv_ref.dtype)
 
     def settle(c):
         r = rows_of[c]
@@ -271,7 +312,7 @@
                 far_sum = sum(box[1, s, r].astype(jnp.float32) for s in range(1, STEPS))
                 side[c].wait_recv()
                 a = total[r].astype(jnp.float32) + near_sum
-                out_ref[r] = (a + (last[r].astype(jnp.float32) + far_sum)).astype(out_ref.dtype)
+                release(r, a + (last[r].astype(jnp.float32) + far_sum))
             else:
                 total[r] = (mine[r] + near_sum).astype(total.dtype)
                 side[c].start()
@@ -303,9 +344,6 @@
     for t in reversed(range(count)):
         begins[t] = len(work)
         work += [((1, t), i) for i in range(t, count)]
-        for c, seg in enumerate(segs):
-            if seg[-1] == t:
-                ends[len(work) - 1] = c
     for c in range(1, len(groups)):
         todo = acts.setdefault(begins[groups[c][0]] - 1, [])
         if c + 1 < len(groups):
@@ -313,6 +351,17 @@
         todo.append(("arrive", c))
         if c == 1:
             todo.append(("mine", tail))
+    early = segs[0][-1] - 1
+    acts.setdefault(begins[early - 1] - 1, []).append(("leave", 0))
+    drained = set()
+    for c in range(1, MERGED + 1):
+        stop = begins[segs[c][-1] - 1] - 1
+        drained.add(stop)
+        acts.setdefault(stop, []).extend([("merge", c - 1), ("leave", c)])
+    for c in range(MERGED + 1, len(segs)):
+        ends_at = begins[segs[c][-1] - 1] - 1 if segs[c][-1] else len(work) - 1
+        ends[ends_at] = c
+
     def act(name, c):
         if name == "note":
             noted.wait_recv()
@@ -328,28 +377,36 @@
             relay(c)
         elif name == "arrive":
             arrive(c)
+        elif name == "leave":
+            leave(c)
         else:
             merge(c)
 
+    def leave(c):
+        if c < MERGED:
+            give[c].start()
+            own[c].start()
+        else:
+            for x in straight[c - MERGED]:
+                x.start()
+
     put(probs(*work[0]), 0)
     for j, (unit, i) in enumerate(work):
+        fresh = j == 0 or work[j - 1][0] != unit
+        done = j + 1 == len(work) or work[j + 1][0] != unit
+        if j in drained:
+            add_grads(unit, i, j % 2, fresh)
+            finish(unit)
         for name, c in acts.get(j, []):
             act(name, c)
         if j + 1 < len(work):
             put(probs(*work[j + 1]), (j + 1) % 2)
-        add_grads(unit, i, j % 2, j == 0 or work[j - 1][0] != unit)
-        if j + 1 == len(work) or work[j + 1][0] != unit:
-            finish(unit)
+        if j not in drained:
+            add_grads(unit, i, j % 2, fresh)
+            if done:
+                finish(unit)
         if j in ends:
-            c = ends[j]
-            if c < MERGED:
-                give[c].start()
-                own[c].start()
-            else:
-                for x in straight[c - MERGED]:
-                    x.start()
-            if 0 < c <= MERGED:
-                merge(c - 1)
+            leave(ends[j])
 
     def write(i):
         r = lanes(i)
@@ -361,7 +418,7 @@
         settle(c)
     for c, r in enumerate(rows_of[:tail]):
         side[c].wait_recv()
-        out_ref[r] = (total[r].astype(jnp.float32) + last[r].astype(jnp.float32)).astype(out_ref.dtype)
+        release(r, total[r].astype(jnp.float32) + last[r].astype(jnp.float32))
     for x in sent:
         x.wait_send()
 
@@ -392,10 +449,11 @@
         functools.partial(kernel, n),
         out_shape=(
             jax.ShapeDtypeStruct(q.shape, q.dtype),
-            jax.ShapeDtypeStruct(pair, low),
+            jax.ShapeDtypeStruct(k.shape, low),
+            jax.ShapeDtypeStruct(v.shape, low),
         ),
         in_specs=[ANY_SPEC] * 8,
-        out_specs=(VMEM_SPEC, VMEM_SPEC),
+        out_specs=(VMEM_SPEC,) * 3,
         scratch_shapes=[
             pltpu.VMEM((STEPS,) + pair, low),
             pltpu.VMEM(q.shape, low),
@@ -426,17 +484,41 @@
     )(k, v, lse, start, pos, q, g, o)
 
 
+def put_kernel(*refs):
+    count = len(refs) // 2
+    sems = refs[-1]
+    moves = [
+        pltpu.make_async_copy(refs[j], refs[count + j], sems.at[j]) for j in range(count)
+    ]
+    for x in moves:
+        x.start()
+    for x in moves:
+        x.wait()
+
+
+def put_out(*arrays):
+    return pl.pallas_call(
+        put_kernel,
+        out_shape=tuple(jax.ShapeDtypeStruct(x.shape, x.dtype) for x in arrays),
+        in_specs=[ANY_SPEC] * len(arrays),
+        out_specs=(pl.BlockSpec(memory_space=pltpu.HBM),) * len(arrays),
+        scratch_shapes=[pltpu.SemaphoreType.DMA((len(arrays),))],
+        compiler_params=pltpu.CompilerParams(vmem_limit_bytes=4 << 20),
+        name="put_out",
+    )(*arrays)
+
+
 def on_device(
     n, queries, out_grad, outputs, key_vectors, value_vectors, logsumexp, positions, doc_start
 ):
     width = queries.shape[-1]
     flat = (-1, width)
-    dq, both = fused(
+    dq, dk, dv = put_out(*fused(
         n, key_vectors, value_vectors, logsumexp.T, doc_start.reshape(1, -1),
         positions.reshape(1, -1), queries.reshape(flat), out_grad.reshape(flat),
         outputs.reshape(flat),
-    )
-    return dq.reshape(queries.shape), both[:, :width], both[:, width:]
+    ))
+    return dq.reshape(queries.shape), dk, dv
 
 
 def solution(mesh):

time: 37 us -> 35.5 us (0.959)
  local copies, waits for them, and re-layouts: 1.69 us -> 0 us
    pallas_call x1, Pallas kernels: 34.5 us -> 33.4 us  [fused(): pl.pallas_call(functools.partial(kernel, n), out_shape=(jax.ShapeDtypeStr...]
    pallas_call x0 -> x1, Pallas kernels: none -> 1.07 us  [put_out(): pl.pallas_call(put_kernel, out_shape=tuple((jax.ShapeDtypeStruct(x.shape,...]
    unnamed x1 -> x0, local copies, waits for them, and re-layouts: 0.97 us -> none
    slice x1 -> x0, local copies, waits for them, and re-layouts: 0.72 us -> none  [on_device(): return (dq.reshape(queries.shape), both[:, :width], both[:, width:])]
where the time goes in v3:
time: 35.5 us; the launch traced here: 35.3 us
  Pallas kernels  34.5 us (97%)
  between operations  0.8 us (2%)
    pallas_call x1, Pallas kernels, fused(): pl.pallas_call(functools.partial(kernel, n), out_shape=(jax.ShapeDtypeStr...  33.4 us
    pallas_call x1, Pallas kernels, put_out(): pl.pallas_call(put_kernel, out_shape=tuple((jax.ShapeDtypeStruct(x.shape,...  1.07 us

profile of v3, /device:TPU:0, one launch (start us, length us, event | category | flops | bytes accessed | tf_op | source)
XLA Modules:
  0.0 35.3 jit_solution(18318549081896874047)
XLA Ops:
  0.6 33.4 %fused_grads.1 = (bf16[4096,128]{1,0:T(8,128)(2,1)S(1)}, bf16[512,128]{1,0:T(8,128)(2,1)S(1)}, bf16[512,128]{1,0:T(8,128)(2,1)S(1)}) custom-call(bf16[512,128]{1,0:T(8,128)(2,1)} %k_hbm.1, bf16[512,128]{1,0:T(8,128)(2,1)} %v_hbm.1, f32[8,512]{1,0:T(8,128)} %bitcast.10, s32[1,512]{1,0:T(1,128)} %bitcast.11, s32[1,512]{1,0:T(1,128)} %bitcast.12, ...), custom_call_target="tpu_custom_call" | custom-call | tf_op jit(solution)/shard_map/fused_grads/pallas_call | solution.py:448
  34.1 1.1 %put_out.1 = (bf16[4096,128]{1,0:T(8,128)(2,1)}, bf16[512,128]{1,0:T(8,128)(2,1)}, bf16[512,128]{1,0:T(8,128)(2,1)}) custom-call(bf16[4096,128]{1,0:T(8,128)(2,1)S(1)} %get-tuple-element.9.refs_0_, bf16[512,128]{1,0:T(8,128)(2,1)S(1)} %get-tuple-element.10.refs_1_, bf16[512,128]{1,0:T(8,128)(2,1)S(1)} %get-tuple-element.11.refs_2_), custom_call_target="tpu_custom_call" | custom-call | tf_op jit(solution)/shard_map/put_out/pallas_call | solution.py:500

commit v4 on v3

--- a/solution.py
+++ b/solution.py
@@ -12,6 +12,7 @@
 TILE = 64
 CHUNK = 128
 MERGED = 2
+SOON = 3
 LOG2E = math.log2(math.e)
 MESH = pl.DeviceIdType.MESH
 VMEM_SPEC = pl.BlockSpec(memory_space=pltpu.VMEM)
@@ -191,11 +192,24 @@
         c.wait()
     for c in note:
         c.start()
+    odd = jnp.logical_not(even)
     first[0].start()
-    for x, y in zip(first[1:], other):
+    for x, y in zip(first[1:SOON], other):
         x.start()
         y.start()
-    other[-1].start()
+
+    @pl.when(even)
+    def _():
+        for x, y in zip(first[SOON:], other[SOON - 1 :]):
+            x.start()
+            y.start()
+        other[-1].start()
+
+    @pl.when(odd)
+    def _():
+        for y in other[SOON - 1 :]:
+            y.start()
+
 
     ramp = lax.broadcasted_iota(jnp.int32, (CHUNK, width), 0) * n
     own_kp[...] = (ramp + pos_ref[0:1, 0:1]).astype(jnp.float32)
@@ -338,7 +352,7 @@
     work, acts, ends = [], {}, {}
     for t in reversed(range(chunks)):
         work += [((0, t), i) for i in range(t * per, count)]
-    acts[len(work) - 1 - count // 2] = [("relay", 0)]
+    acts[len(work) - 1 - count // 2] = [("later", 0), ("relay", 0)]
     acts[len(work) - 1] = [("note", 0), ("relay", 1), ("arrive", 0)]
     begins = {}
     for t in reversed(range(count)):
@@ -369,6 +383,13 @@
                 kp_buf[(s - 1) * TILE : s * TILE, :] = (
                     ramp[:TILE] + marks[s, 0:1, 0:1]
                 ).astype(jnp.float32)
+        elif name == "later":
+
+            @pl.when(odd)
+            def _():
+                for x in first[SOON:]:
+                    x.start()
+
         elif name == "mine":
             r = rows_of[c]
             total[r] = mine[r].astype(total.dtype)
@@ -412,9 +433,11 @@
         r = lanes(i)
         dq_ref[r, :] = (dq_acc[:, r].T * scaling).astype(dq_ref.dtype)
 
+    for c in range(MERGED):
+        settle(c)
     for i in range(count):
         write(i)
-    for c in range(tail + 1):
+    for c in range(MERGED, tail + 1):
         settle(c)
     for c, r in enumerate(rows_of[:tail]):
         side[c].wait_recv()

time: 35.5 us -> 34.8 us (0.980)
  Pallas kernels: 34.5 us -> 33.8 us
    pallas_call x1, Pallas kernels: 33.4 us -> 32.8 us  [fused(): pl.pallas_call(functools.partial(kernel, n), out_shape=(jax.ShapeDtypeStr...]
where the time goes in v4:
time: 34.8 us; the launch traced here: 34.6 us
  Pallas kernels  33.8 us (97%)
  between operations  0.8 us (2%)
    pallas_call x1, Pallas kernels, fused(): pl.pallas_call(functools.partial(kernel, n), out_shape=(jax.ShapeDtypeStr...  32.8 us
    pallas_call x1, Pallas kernels, put_out(): pl.pallas_call(put_kernel, out_shape=tuple((jax.ShapeDtypeStruct(x.shape,...  1.07 us

profile of v4, /device:TPU:0, one launch (start us, length us, event | category | flops | bytes accessed | tf_op | source)
XLA Modules:
  0.0 34.6 jit_solution(17499730646421529331)
XLA Ops:
  0.6 32.8 %fused_grads.1 = (bf16[4096,128]{1,0:T(8,128)(2,1)S(1)}, bf16[512,128]{1,0:T(8,128)(2,1)S(1)}, bf16[512,128]{1,0:T(8,128)(2,1)S(1)}) custom-call(bf16[512,128]{1,0:T(8,128)(2,1)} %k_hbm.1, bf16[512,128]{1,0:T(8,128)(2,1)} %v_hbm.1, f32[8,512]{1,0:T(8,128)} %bitcast.10, s32[1,512]{1,0:T(1,128)} %bitcast.11, s32[1,512]{1,0:T(1,128)} %bitcast.12, ...), custom_call_target="tpu_custom_call" | custom-call | tf_op jit(solution)/shard_map/fused_grads/pallas_call | solution.py:471
  33.4 1.1 %put_out.1 = (bf16[4096,128]{1,0:T(8,128)(2,1)}, bf16[512,128]{1,0:T(8,128)(2,1)}, bf16[512,128]{1,0:T(8,128)(2,1)}) custom-call(bf16[4096,128]{1,0:T(8,128)(2,1)S(1)} %get-tuple-element.9.refs_0_, bf16[512,128]{1,0:T(8,128)(2,1)S(1)} %get-tuple-element.10.refs_1_, bf16[512,128]{1,0:T(8,128)(2,1)S(1)} %get-tuple-element.11.refs_2_), custom_call_target="tpu_custom_call" | custom-call | tf_op jit(solution)/shard_map/put_out/pallas_call | solution.py:523
